TPU v7x, 512 devices: a whole 4x8x8 slice. The times are simulated.
512 devices in a mesh: seq: 256 (over z, x, y_lo, core), head: 2 (over y_hi).
Axes of the slice: x: 4, y: 8 (y_hi: 2, y_lo: 4; y = y_hi * 4 + y_lo), z: 8, core: 2. Of those that a mesh axis runs over, the one named last changes fastest.
Arguments:
- queries: bfloat16 [32768, 2048], P('seq', 'head'), may hold values from -5 to 5
- keys: bfloat16 [32768, 2048], P('seq', 'head'), may hold values from -5 to 5
- values: bfloat16 [32768, 2048], P('seq', 'head'), may hold values from -6 to 6
- grad_out: bfloat16 [32768, 2048], P('seq', 'head'), may hold values from -6 to 6
- doc_ids: int32 [32768], P(('seq', 'head')), may hold values from 0 to 511, never falling along the last dimension, each value on 1 to 512 neighbouring positions
- loss_mask: int32 [32768], P(('seq', 'head')), may hold values 0 or 1
Outputs:
- attended: bfloat16 [32768, 2048], P('seq', 'head')
- query_grad: bfloat16 [32768, 2048], P('seq', 'head')
- key_grad: bfloat16 [32768, 2048], P('seq', 'head')
- value_grad: bfloat16 [32768, 2048], P('seq', 'head')
Inputs may be any that keep to these rules, and one draw needn't show every extreme that they name: `doc_ids`: documents are runs of consecutive tokens numbered 0, 1, 2, ... in order; each has 1 to 512 tokens.
All inputs are finite; a program needn't handle non-finite values. No bound on the sum of `loss_mask` on one device may be relied on, other than what follows from the above.
Results may differ from a plain program's by a relative error of at most 0.033.
Values may be sent and summed in bfloat16 or wider, within the bound.
A program may use at most 64 MiB of HBM per device.

v0:
```python
from functools import reduce
import math
import jax
import jax.numpy as jnp
from jax import lax
from jax.sharding import Mesh
from jax.sharding import PartitionSpec as P

HEAD_DIM = 128
REACH = 4
WINDOW = 512
SEQ = ("seq_0", "seq_1", "seq_2", "seq_3")
SEQ_HEAD = ("seq_0", "seq_1", "seq_2", "seq_3", "head")
masked_value = -1e30
big_index = 2**30


def turned_gather(arrays, axis, dims):
    turned = [jnp.moveaxis(a, dim, 0) for a, dim in zip(arrays, dims)]
    widths = [t[0].size for t in turned]
    both = jnp.concatenate([t.reshape(-1, w) for t, w in zip(turned, widths)], axis=1)
    out = lax.all_gather(both, axis, axis=0, tiled=True)
    pieces = jnp.split(out, [sum(widths[:k]) for k in range(1, len(widths))], axis=1)
    return tuple(
        (
            jnp.moveaxis(b.reshape(-1, *t.shape[1:]), 0, dim)
            for b, t, dim in zip(pieces, turned, dims)
        )
    )


def by_axis(value, axes):
    for axis in axes:
        value = lax.psum(value, axis)
    return value


def one_axis_at_a_time(value, axes):
    for axis in axes:
        value = lax.pmin(value, axis)
    return value


def shifted(block, axis, distance):
    devices = range(lax.axis_size(axis))
    route = [(i - distance, i) for i in devices if i - distance in devices]
    return lax.ppermute(block, axis, route)


def for_sending(value):

    def short(part):
        return part.astype(jnp.bfloat16) if part.dtype == jnp.float32 else part

    return jax.tree.map(short, value)


def allowed_for(q_pos, q_start, k_pos):
    later = k_pos[None, :] <= q_pos[:, None]
    inside = k_pos[None, :] > q_pos[:, None] - WINDOW
    same_doc = k_pos[None, :] >= q_start[:, None]
    return later & inside & same_doc


def by_head(rows):
    return rows.reshape(rows.shape[0], -1, HEAD_DIM)


def tile_scores(q_rows, k_rows, allowed):
    score = jnp.einsum(
        "qhd,khd->hqk", by_head(q_rows), by_head(k_rows), preferred_element_type=jnp.float32
    )
    return jnp.where(allowed[None], score * (1.0 / math.sqrt(HEAD_DIM)), masked_value)


def tile_mix(prob, v_rows):
    return jnp.einsum(
        "hqk,khd->qhd",
        prob.astype(jnp.bfloat16),
        by_head(v_rows),
        preferred_element_type=jnp.float32,
    )


def grad_of_scores(g_rows, v_rows, prob, row_delta):
    prob_grad = jnp.einsum(
        "qhd,khd->hqk", by_head(g_rows), by_head(v_rows), preferred_element_type=jnp.float32
    )
    return (prob * (prob_grad - row_delta[..., None]) * (1.0 / math.sqrt(HEAD_DIM))).astype(
        jnp.bfloat16
    )


def key_terms_of(q_rows, g_rows, k_rows, prob, score_grad):
    key_part = jnp.einsum(
        "hqk,qhd->khd", score_grad, by_head(q_rows), preferred_element_type=jnp.float32
    )
    value_part = jnp.einsum(
        "hqk,qhd->khd",
        prob.astype(jnp.bfloat16),
        by_head(g_rows),
        preferred_element_type=jnp.float32,
    )
    return (key_part.reshape(k_rows.shape), value_part.reshape(k_rows.shape))


def tile_back(q_rows, g_rows, k_rows, v_rows, prob, row_delta):
    score_grad = grad_of_scores(g_rows, v_rows, prob, row_delta)
    result = jnp.einsum(
        "hqk,khd->qhd", score_grad, by_head(k_rows), preferred_element_type=jnp.float32
    )
    key_part, value_part = key_terms_of(q_rows, g_rows, k_rows, prob, score_grad)
    return (result.reshape(q_rows.shape), key_part, value_part)


def body(queries, keys, values, grad_out, doc_ids, loss_mask):
    block_rows, width = queries.shape
    seq_index = lax.axis_index(SEQ)
    doc_rows, mask_rows = turned_gather((doc_ids, loss_mask), "head", (0, 0))
    positions = seq_index * block_rows + jnp.arange(block_rows, dtype=jnp.int32)
    catalog = jnp.arange(2 * lax.axis_size(SEQ), dtype=jnp.int32)
    member = doc_rows[:, None] == catalog[None, :]
    local_counts = jnp.sum(jnp.where(member, mask_rows[:, None].astype(jnp.float32), 0.0), axis=0)
    local_first = jnp.min(jnp.where(member, positions[:, None], big_index), axis=0)
    counts = by_axis(local_counts, SEQ)
    firsts = one_axis_at_a_time(local_first, SEQ)
    doc_start = jnp.sum(jnp.where(member, firsts[None, :], 0), axis=1)
    doc_count = jnp.sum(jnp.where(member, counts[None, :], 0.0), axis=1)
    weight = (
        mask_rows.astype(jnp.float32) * block_rows / jnp.maximum(doc_count, float(block_rows // 8))
    )
    remote = []
    carried = (keys, values)
    for distance in range(1, REACH + 1):
        carried = shifted((carried[0], carried[1]), SEQ, 1)
        remote.append(carried)
    key_blocks = [(keys, values)] + remote
    masks = [
        allowed_for(positions, doc_start, positions - distance * block_rows)
        for distance in range(REACH + 1)
    ]
    score_list = [
        tile_scores(queries, key_blocks[distance][0], masks[distance])
        for distance in range(REACH + 1)
    ]
    row_max = reduce(jnp.maximum, [jnp.max(score, axis=2) for score in score_list])
    row_sum = sum((jnp.sum(jnp.exp(score - row_max[..., None]), axis=2) for score in score_list))
    log_total = row_max + jnp.log(row_sum)
    prob_list = [jnp.exp(score - log_total[..., None]) for score in score_list]
    mixed_out = sum(
        (tile_mix(prob_list[distance], key_blocks[distance][1]) for distance in range(REACH + 1))
    )
    attended = mixed_out.astype(jnp.bfloat16).reshape(block_rows, width)
    grad_rows = (weight[:, None] * grad_out.astype(jnp.float32)).astype(jnp.bfloat16)
    row_delta = jnp.sum(
        by_head(grad_rows).astype(jnp.float32) * by_head(attended).astype(jnp.float32), axis=2
    ).T
    terms = [
        tile_back(
            queries,
            grad_rows,
            key_blocks[distance][0],
            key_blocks[distance][1],
            prob_list[distance],
            row_delta,
        )
        for distance in range(REACH + 1)
    ]
    query_total = sum((term[0] for term in terms))
    carried = (terms[REACH][1], terms[REACH][2])
    for distance in range(REACH - 1, -1, -1):
        carried = shifted((for_sending(carried[0]), for_sending(carried[1])), SEQ, -1)
        carried = (carried[0] + terms[distance][1], carried[1] + terms[distance][2])
    return (
        attended,
        query_total.astype(jnp.bfloat16),
        carried[0].astype(jnp.bfloat16),
        carried[1].astype(jnp.bfloat16),
    )


def solution(mesh):
    torus = Mesh(
        mesh.devices.reshape(8, 4, 4, 2, mesh.shape["head"]),
        ("seq_0", "seq_1", "seq_2", "seq_3", "head"),
    )
    in_specs = (
        P(SEQ, "head"),
        P(SEQ, "head"),
        P(SEQ, "head"),
        P(SEQ, "head"),
        P(SEQ_HEAD),
        P(SEQ_HEAD),
    )
    out_specs = (P(SEQ, "head"), P(SEQ, "head"), P(SEQ, "head"), P(SEQ, "head"))
    return jax.shard_map(body, mesh=torus, in_specs=in_specs, out_specs=out_specs, check_vma=False)
```

profile of v0, /device:TPU:255, one launch (start us, length us, event | category | flops | bytes accessed | tf_op | source)
XLA Modules:
  0.0 208.5 jit_solution(2514917617455026863)
XLA Ops:
  1.8 8.0 %collective-permute-start = (bf16[128,1024]{0,1:T(8,128)(2,1)S(1)}, bf16[128,1024]{0,1:T(8,128)(2,1)S(1)}, u32[]{:S(2)}, u32[]{:S(2)}) collective-permute-start(bf16[128,1024]{0,1:T(8,128)(2,1)S(1)} %copy.331), channel_id=1, source_target_pairs={{0,2},{2,4},{4,6},{6,8},{8,10},{10,12},{12,14},{14,16},{16,18},{18... | collective-permute-start | bytes 786440 | tf_op jit(solution)/shard_map/ppermute | solution.py:47
  12.6 7.0 %all-gather = s32[2,64,2]{1,2,0:T(2,128)S(1)} all-gather(s32[1,64,2]{1,2,0:T(2,128)S(1)} %add_bitcast_fusion), channel_id=1, replica_groups=mesh['seq_0'=8,'seq_1'=4,'seq_2'=4,'seq_3'=2,'head'=2] {'head'}, dimensions={0}, use_global_device_ids=true | all-gather | bytes 1536 | tf_op jit(solution)/shard_map/all_gather | solution.py:22
  19.8 9.4 %pmin.28 = s32[512]{0:T(512)S(1)} all-reduce(s32[512]{0:T(512)S(1)} %select_reduce_fusion.3), channel_id=1, replica_groups=mesh['seq_0'=8,'seq_1'=4,'seq_2'=4,'seq_3'=2,'head'=2] {'seq_0'}, use_global_device_ids=true, to_apply=%region_1.2 | all-reduce | flops 512 | bytes 4096 | tf_op jit(solution)/shard_map/pmin | solution.py:40
  29.1 5.7 %pmin.29 = s32[512]{0:T(512)S(1)} all-reduce(s32[512]{0:T(512)S(1)} %pmin.28), channel_id=1, replica_groups=mesh['seq_0'=8,'seq_1'=4,'seq_2'=4,'seq_3'=2,'head'=2] {'seq_1'}, use_global_device_ids=true, to_apply=%region_2.3 | all-reduce | flops 512 | bytes 4096 | tf_op jit(solution)/shard_map/pmin | solution.py:40
  34.8 4.0 %pmin.30 = s32[512]{0:T(512)S(1)} all-reduce(s32[512]{0:T(512)S(1)} %pmin.29), channel_id=1, replica_groups=mesh['seq_0'=8,'seq_1'=4,'seq_2'=4,'seq_3'=2,'head'=2] {'seq_2'}, use_global_device_ids=true, to_apply=%region_3.4 | all-reduce | flops 512 | bytes 4096 | tf_op jit(solution)/shard_map/pmin | solution.py:40
  38.8 9.3 %pmin.31 = s32[512]{0:T(512)S(1)} all-reduce(s32[512]{0:T(512)S(1)} %pmin.30), channel_id=1, replica_groups=mesh['seq_0'=8,'seq_1'=4,'seq_2'=4,'seq_3'=2,'head'=2] {'seq_3'}, use_global_device_ids=true, to_apply=%region_4.5 | all-reduce | flops 512 | bytes 4096 | tf_op jit(solution)/shard_map/pmin | solution.py:40
  48.8 10.6 %psum.28 = f32[512]{0:T(512)S(1)} all-reduce(f32[512]{0:T(512)S(1)} %select_reduce_fusion.1), channel_id=1, replica_groups=mesh['seq_0'=8,'seq_1'=4,'seq_2'=4,'seq_3'=2,'head'=2] {'seq_0'}, use_global_device_ids=true, to_apply=%region_17.18 | all-reduce | flops 512 | bytes 4096 | tf_op jit(solution)/shard_map/psum | solution.py:34
  59.4 6.3 %psum.29 = f32[512]{0:T(512)S(1)} all-reduce(f32[512]{0:T(512)S(1)} %psum.28), channel_id=1, replica_groups=mesh['seq_0'=8,'seq_1'=4,'seq_2'=4,'seq_3'=2,'head'=2] {'seq_1'}, use_global_device_ids=true, to_apply=%region_18.19 | all-reduce | flops 512 | bytes 4096 | tf_op jit(solution)/shard_map/psum | solution.py:34
  65.6 7.3 %psum.30 = f32[512]{0:T(512)S(1)} all-reduce(f32[512]{0:T(512)S(1)} %psum.29), channel_id=1, replica_groups=mesh['seq_0'=8,'seq_1'=4,'seq_2'=4,'seq_3'=2,'head'=2] {'seq_2'}, use_global_device_ids=true, to_apply=%region_19.20 | all-reduce | flops 512 | bytes 4096 | tf_op jit(solution)/shard_map/psum | solution.py:34
  72.9 10.1 %psum.31 = f32[512]{0:T(512)S(1)} all-reduce(f32[512]{0:T(512)S(1)} %psum.30), channel_id=1, replica_groups=mesh['seq_0'=8,'seq_1'=4,'seq_2'=4,'seq_3'=2,'head'=2] {'seq_3'}, use_global_device_ids=true, to_apply=%region_20.21 | all-reduce | flops 512 | bytes 4096 | tf_op jit(solution)/shard_map/psum | solution.py:34
  83.4 10.3 %collective-permute-start.1 = (bf16[128,1024]{0,1:T(8,128)(2,1)S(1)}, bf16[128,1024]{0,1:T(8,128)(2,1)S(1)}, u32[]{:S(2)}, u32[]{:S(2)}) collective-permute-start(bf16[128,1024]{0,1:T(8,128)(2,1)S(1)} %collective-permute-done), channel_id=1, source_target_pairs={{0,2},{2,4},{4,6},{6,8},{8,10},{10,12},{12,14},{14,16},{16,18},{18... | collective-permute-start | bytes 786440 | tf_op jit(solution)/shard_map/ppermute | solution.py:47
  93.8 2.1 collective-permute-start.5
  96.9 10.4 %collective-permute-start.2 = (bf16[128,1024]{0,1:T(8,128)(2,1)S(1)}, bf16[128,1024]{0,1:T(8,128)(2,1)}, u32[]{:S(2)}, u32[]{:S(2)}) collective-permute-start(bf16[128,1024]{0,1:T(8,128)(2,1)S(1)} %collective-permute-done.1), channel_id=1, source_target_pairs={{0,2},{2,4},{4,6},{6,8},{8,10},{10,12},{12,14},{14,16},{16,18},{18... | collective-permute-start | bytes 786440 | tf_op jit(solution)/shard_map/ppermute | solution.py:47
  107.6 2.5 %collective-permute-start.6 = (bf16[128,1024]{1,0:T(8,128)(2,1)S(1)}, bf16[128,1024]{1,0:T(8,128)(2,1)}, u32[]{:S(2)}, u32[]{:S(2)}) collective-permute-start(bf16[128,1024]{1,0:T(8,128)(2,1)S(1)} %collective-permute-done.5), channel_id=1, source_target_pairs={{0,2},{2,4},{4,6},{6,8},{8,10},{10,12},{12,14},{14,16},{16,18},{18... | collective-permute-start | bytes 786440 | tf_op jit(solution)/shard_map/ppermute | solution.py:47
  110.6 10.5 %collective-permute-start.3 = (bf16[128,1024]{0,1:T(8,128)(2,1)}, bf16[128,1024]{0,1:T(8,128)(2,1)S(1)}, u32[]{:S(2)}, u32[]{:S(2)}) collective-permute-start(bf16[128,1024]{0,1:T(8,128)(2,1)} %collective-permute-done.2), channel_id=1, source_target_pairs={{0,2},{2,4},{4,6},{6,8},{8,10},{10,12},{12,14},{14,16},{16,18},{18... | collective-permute-start | bytes 786440 | tf_op jit(solution)/shard_map/ppermute | solution.py:47
  135.2 2.1 %multiply_reduce_fusion = (f32[128,8]{0,1:T(8,128)S(1)}, bf16[8,128,128]{1,2,0:T(8,128)(2,1)}) fusion(bf16[128,1024]{0,1:T(8,128)(2,1)S(1)} %copy.243, f32[8,128,128]{1,2,0:T(8,128)} %convolution_add_fusion.5, bf16[128,8,128]{0,2,1:T(8,128)(2,1)} %bitcast.152, f32[8,128,128]{1,2,0:T(8,128)S(1)} %get-tuple-element.33, f32[8,128]{1,0:T(8,128)S(1)} %log_add_fusion), kind=kOutput, calls=%fused_computation.50 | convolution fusion | flops 34601984 | bytes 1843200 | tf_op jit(solution)/shard_map/hqk,khd->qhd/dot_general | solution.py:77
  149.4 2.4 %collective-permute-start.8 = (bf16[128,1024]{1,0:T(8,128)(2,1)S(1)}, bf16[128,1024]{1,0:T(8,128)(2,1)S(1)}, u32[]{:S(2)}, u32[]{:S(2)}) collective-permute-start(bf16[128,1024]{1,0:T(8,128)(2,1)S(1)} %copy.267), channel_id=1, source_target_pairs={{2,0},{4,2},{6,4},{8,6},{10,8},{12,10},{14,12},{16,14},{18,16},{20... | collective-permute-start | bytes 786440 | tf_op jit(solution)/shard_map/ppermute | solution.py:47
  155.8 7.3 %collective-permute-done.8 = bf16[128,1024]{1,0:T(8,128)(2,1)S(1)} collective-permute-done((bf16[128,1024]{1,0:T(8,128)(2,1)S(1)}, bf16[128,1024]{1,0:T(8,128)(2,1)S(1)}, u32[]{:S(2)}, u32[]{:S(2)}) %collective-permute-start.8) | collective-permute-done | bytes 262176 | tf_op jit(solution)/shard_map/ppermute | solution.py:47
  163.2 2.1 collective-permute-start.9
  169.6 7.5 %collective-permute-done.9 = bf16[128,1024]{1,0:T(8,128)(2,1)S(1)} collective-permute-done((bf16[128,1024]{1,0:T(8,128)(2,1)S(1)}, bf16[128,1024]{1,0:T(8,128)(2,1)S(1)}, u32[]{:S(2)}, u32[]{:S(2)}) %collective-permute-start.9) | collective-permute-done | bytes 262176 | tf_op jit(solution)/shard_map/ppermute | solution.py:47
  177.1 2.1 collective-permute-start.10
  183.4 7.6 %collective-permute-done.10 = bf16[128,1024]{1,0:T(8,128)(2,1)S(1)} collective-permute-done((bf16[128,1024]{1,0:T(8,128)(2,1)S(1)}, bf16[128,1024]{1,0:T(8,128)(2,1)S(1)}, u32[]{:S(2)}, u32[]{:S(2)}) %collective-permute-start.10) | collective-permute-done | bytes 262176 | tf_op jit(solution)/shard_map/ppermute | solution.py:47
  191.0 2.1 collective-permute-start.11
  199.2 5.7 %collective-permute-done.11 = bf16[128,1024]{1,0:T(8,128)(2,1)S(1)} collective-permute-done((bf16[128,1024]{1,0:T(8,128)(2,1)S(1)}, bf16[128,1024]{1,0:T(8,128)(2,1)S(1)}, u32[]{:S(2)}, u32[]{:S(2)}) %collective-permute-start.11) | collective-permute-done | bytes 262176 | tf_op jit(solution)/shard_map/ppermute | solution.py:47
  (157 shorter events, 54.9 us)
Async XLA Ops:
  0.6 9.3 %copy-start.19 = (bf16[128,1024]{1,0:T(8,128)(2,1)S(1)}, bf16[128,1024]{1,0:T(8,128)(2,1)}, u32[]{:S(2)}) copy-start(bf16[128,1024]{1,0:T(8,128)(2,1)} %param.8) | copy-start | bytes 786436
  0.6 48.0 %copy-start.30 = (bf16[128,1024]{1,0:T(8,128)(2,1)S(1)}, bf16[128,1024]{1,0:T(8,128)(2,1)}, u32[]{:S(2)}) copy-start(bf16[128,1024]{1,0:T(8,128)(2,1)} %param.6) | copy-start | bytes 786436
  1.8 81.2 %copy-start.13 = (bf16[128,1024]{0,1:T(8,128)(2,1)}, bf16[128,1024]{0,1:T(8,128)(2,1)S(1)}, u32[]{:S(2)}) copy-start(bf16[128,1024]{0,1:T(8,128)(2,1)S(1)} %copy.331) | copy-start | bytes 786436
  1.8 81.5 %collective-permute-start = (bf16[128,1024]{0,1:T(8,128)(2,1)S(1)}, bf16[128,1024]{0,1:T(8,128)(2,1)S(1)}, u32[]{:S(2)}, u32[]{:S(2)}) collective-permute-start(bf16[128,1024]{0,1:T(8,128)(2,1)S(1)} %copy.331), channel_id=1, source_target_pairs={{0,2},{2,4},{4,6},{6,8},{8,10},{10,12},{12,14},{14,16},{16,18},{18... | collective-permute-start | bytes 786440 | tf_op jit(solution)/shard_map/ppermute | solution.py:47
  9.9 83.9 %collective-permute-start.4 = (bf16[128,1024]{1,0:T(8,128)(2,1)S(1)}, bf16[128,1024]{1,0:T(8,128)(2,1)S(1)}, u32[]{:S(2)}, u32[]{:S(2)}) collective-permute-start(bf16[128,1024]{1,0:T(8,128)(2,1)S(1)} %copy-done.19), channel_id=1, source_target_pairs={{0,2},{2,4},{4,6},{6,8},{8,10},{10,12},{12,14},{14,16},{16,18},{18... | collective-permute-start | bytes 786440 | tf_op jit(solution)/shard_map/ppermute | solution.py:47
  83.0 24.3 %copy-start.29 = (bf16[128,1024]{1,0:T(8,128)(2,1)S(1)}, bf16[128,1024]{1,0:T(8,128)(2,1)}, u32[]{:S(2)}) copy-start(bf16[128,1024]{1,0:T(8,128)(2,1)} %param.9) | copy-start | bytes 786436
  83.3 26.8 %copy-start.25 = (bf16[128,1024]{0,1:T(8,128)(2,1)}, bf16[128,1024]{0,1:T(8,128)(2,1)S(1)}, u32[]{:S(2)}) copy-start(bf16[128,1024]{0,1:T(8,128)(2,1)S(1)} %collective-permute-done) | copy-start | bytes 786436
  83.4 13.6 %collective-permute-start.1 = (bf16[128,1024]{0,1:T(8,128)(2,1)S(1)}, bf16[128,1024]{0,1:T(8,128)(2,1)S(1)}, u32[]{:S(2)}, u32[]{:S(2)}) collective-permute-start(bf16[128,1024]{0,1:T(8,128)(2,1)S(1)} %collective-permute-done), channel_id=1, source_target_pairs={{0,2},{2,4},{4,6},{6,8},{8,10},{10,12},{12,14},{14,16},{16,18},{18... | collective-permute-start | bytes 786440 | tf_op jit(solution)/shard_map/ppermute | solution.py:47
  93.8 13.8 %collective-permute-start.5 = (bf16[128,1024]{1,0:T(8,128)(2,1)S(1)}, bf16[128,1024]{1,0:T(8,128)(2,1)S(1)}, u32[]{:S(2)}, u32[]{:S(2)}) collective-permute-start(bf16[128,1024]{1,0:T(8,128)(2,1)S(1)} %collective-permute-done.4), channel_id=1, source_target_pairs={{0,2},{2,4},{4,6},{6,8},{8,10},{10,12},{12,14},{14,16},{16,18},{18... | collective-permute-start | bytes 786440 | tf_op jit(solution)/shard_map/ppermute | solution.py:47
  96.9 24.2 %copy-start.27 = (bf16[128,1024]{0,1:T(8,128)(2,1)}, bf16[128,1024]{0,1:T(8,128)(2,1)S(1)}, u32[]{:S(2)}) copy-start(bf16[128,1024]{0,1:T(8,128)(2,1)S(1)} %collective-permute-done.1) | copy-start | bytes 786436
  96.9 13.7 %collective-permute-start.2 = (bf16[128,1024]{0,1:T(8,128)(2,1)S(1)}, bf16[128,1024]{0,1:T(8,128)(2,1)}, u32[]{:S(2)}, u32[]{:S(2)}) collective-permute-start(bf16[128,1024]{0,1:T(8,128)(2,1)S(1)} %collective-permute-done.1), channel_id=1, source_target_pairs={{0,2},{2,4},{4,6},{6,8},{8,10},{10,12},{12,14},{14,16},{16,18},{18... | collective-permute-start | bytes 786440 | tf_op jit(solution)/shard_map/ppermute | solution.py:47
  107.6 14.6 %collective-permute-start.6 = (bf16[128,1024]{1,0:T(8,128)(2,1)S(1)}, bf16[128,1024]{1,0:T(8,128)(2,1)}, u32[]{:S(2)}, u32[]{:S(2)}) collective-permute-start(bf16[128,1024]{1,0:T(8,128)(2,1)S(1)} %collective-permute-done.5), channel_id=1, source_target_pairs={{0,2},{2,4},{4,6},{6,8},{8,10},{10,12},{12,14},{14,16},{16,18},{18... | collective-permute-start | bytes 786440 | tf_op jit(solution)/shard_map/ppermute | solution.py:47
  110.6 16.6 %collective-permute-start.3 = (bf16[128,1024]{0,1:T(8,128)(2,1)}, bf16[128,1024]{0,1:T(8,128)(2,1)S(1)}, u32[]{:S(2)}, u32[]{:S(2)}) collective-permute-start(bf16[128,1024]{0,1:T(8,128)(2,1)} %collective-permute-done.2), channel_id=1, source_target_pairs={{0,2},{2,4},{4,6},{6,8},{8,10},{10,12},{12,14},{14,16},{16,18},{18... | collective-permute-start | bytes 786440 | tf_op jit(solution)/shard_map/ppermute | solution.py:47
  124.1 9.3 %collective-permute-start.7 = (bf16[128,1024]{1,0:T(8,128)(2,1)}, bf16[128,1024]{1,0:T(8,128)(2,1)}, u32[]{:S(2)}, u32[]{:S(2)}) collective-permute-start(bf16[128,1024]{1,0:T(8,128)(2,1)} %collective-permute-done.6), channel_id=1, source_target_pairs={{0,2},{2,4},{4,6},{6,8},{8,10},{10,12},{12,14},{14,16},{16,18},{18... | collective-permute-start | bytes 786440 | tf_op jit(solution)/shard_map/ppermute | solution.py:47
  137.5 7.9 %copy-start.5 = (bf16[8,128,128]{1,2,0:T(8,128)(2,1)}, bf16[8,128,128]{1,2,0:T(8,128)(2,1)S(1)}, u32[]{:S(2)}) copy-start(bf16[8,128,128]{1,2,0:T(8,128)(2,1)S(1)} %fusion.19) | copy-start | bytes 786436
  138.6 7.4 %copy-start.7 = (bf16[8,128,128]{1,2,0:T(8,128)(2,1)}, bf16[8,128,128]{1,2,0:T(8,128)(2,1)S(1)}, u32[]{:S(2)}) copy-start(bf16[8,128,128]{1,2,0:T(8,128)(2,1)S(1)} %fusion.15) | copy-start | bytes 786436
  149.4 13.7 %collective-permute-start.8 = (bf16[128,1024]{1,0:T(8,128)(2,1)S(1)}, bf16[128,1024]{1,0:T(8,128)(2,1)S(1)}, u32[]{:S(2)}, u32[]{:S(2)}) collective-permute-start(bf16[128,1024]{1,0:T(8,128)(2,1)S(1)} %copy.267), channel_id=1, source_target_pairs={{2,0},{4,2},{6,4},{8,6},{10,8},{12,10},{14,12},{16,14},{18,16},{20... | collective-permute-start | bytes 786440 | tf_op jit(solution)/shard_map/ppermute | solution.py:47
  152.3 13.7 %collective-permute-start.12 = (bf16[128,1024]{1,0:T(8,128)(2,1)S(1)}, bf16[128,1024]{1,0:T(8,128)(2,1)S(1)}, u32[]{:S(2)}, u32[]{:S(2)}) collective-permute-start(bf16[128,1024]{1,0:T(8,128)(2,1)S(1)} %copy.281), channel_id=1, source_target_pairs={{2,0},{4,2},{6,4},{8,6},{10,8},{12,10},{14,12},{16,14},{18,16},{20... | collective-permute-start | bytes 786440 | tf_op jit(solution)/shard_map/ppermute | solution.py:47
  163.2 13.8 %collective-permute-start.9 = (bf16[128,1024]{1,0:T(8,128)(2,1)S(1)}, bf16[128,1024]{1,0:T(8,128)(2,1)S(1)}, u32[]{:S(2)}, u32[]{:S(2)}) collective-permute-start(bf16[128,1024]{1,0:T(8,128)(2,1)S(1)} %add_convert_fusion.7), channel_id=1, source_target_pairs={{2,0},{4,2},{6,4},{8,6},{10,8},{12,10},{14,12},{16,14},{18,16},{20... | collective-permute-start | bytes 786440 | tf_op jit(solution)/shard_map/ppermute | solution.py:47
  166.1 13.8 %collective-permute-start.13 = (bf16[128,1024]{1,0:T(8,128)(2,1)S(1)}, bf16[128,1024]{1,0:T(8,128)(2,1)S(1)}, u32[]{:S(2)}, u32[]{:S(2)}) collective-permute-start(bf16[128,1024]{1,0:T(8,128)(2,1)S(1)} %add_convert_fusion.3), channel_id=1, source_target_pairs={{2,0},{4,2},{6,4},{8,6},{10,8},{12,10},{14,12},{16,14},{18,16},{20... | collective-permute-start | bytes 786440 | tf_op jit(solution)/shard_map/ppermute | solution.py:47
  177.1 13.8 %collective-permute-start.10 = (bf16[128,1024]{1,0:T(8,128)(2,1)S(1)}, bf16[128,1024]{1,0:T(8,128)(2,1)S(1)}, u32[]{:S(2)}, u32[]{:S(2)}) collective-permute-start(bf16[128,1024]{1,0:T(8,128)(2,1)S(1)} %add_convert_fusion.6), channel_id=1, source_target_pairs={{2,0},{4,2},{6,4},{8,6},{10,8},{12,10},{14,12},{16,14},{18,16},{20... | collective-permute-start | bytes 786440 | tf_op jit(solution)/shard_map/ppermute | solution.py:47
  179.9 13.9 %collective-permute-start.14 = (bf16[128,1024]{1,0:T(8,128)(2,1)S(1)}, bf16[128,1024]{1,0:T(8,128)(2,1)S(1)}, u32[]{:S(2)}, u32[]{:S(2)}) collective-permute-start(bf16[128,1024]{1,0:T(8,128)(2,1)S(1)} %add_convert_fusion.2), channel_id=1, source_target_pairs={{2,0},{4,2},{6,4},{8,6},{10,8},{12,10},{14,12},{16,14},{18,16},{20... | collective-permute-start | bytes 786440 | tf_op jit(solution)/shard_map/ppermute | solution.py:47
  191.0 13.8 %collective-permute-start.11 = (bf16[128,1024]{1,0:T(8,128)(2,1)S(1)}, bf16[128,1024]{1,0:T(8,128)(2,1)S(1)}, u32[]{:S(2)}, u32[]{:S(2)}) collective-permute-start(bf16[128,1024]{1,0:T(8,128)(2,1)S(1)} %add_convert_fusion.5), channel_id=1, source_target_pairs={{2,0},{4,2},{6,4},{8,6},{10,8},{12,10},{14,12},{16,14},{18,16},{20... | collective-permute-start | bytes 786440 | tf_op jit(solution)/shard_map/ppermute | solution.py:47
  193.9 13.8 %collective-permute-start.15 = (bf16[128,1024]{1,0:T(8,128)(2,1)S(1)}, bf16[128,1024]{1,0:T(8,128)(2,1)S(1)}, u32[]{:S(2)}, u32[]{:S(2)}) collective-permute-start(bf16[128,1024]{1,0:T(8,128)(2,1)S(1)} %add_convert_fusion.1), channel_id=1, source_target_pairs={{2,0},{4,2},{6,4},{8,6},{10,8},{12,10},{14,12},{16,14},{18,16},{20... | collective-permute-start | bytes 786440 | tf_op jit(solution)/shard_map/ppermute | solution.py:47
  (25 other events, 51.8 us)
where the time goes:
time: 210 us; the launch traced here: 208 us
  blocking collectives  69.6 us (33%)
  starting transfers between devices  64 us (30%)
  waiting for transfers between devices  33.2 us (16%)
  local copies, waits for them, and re-layouts  20 us (10%)
  matrix products  17 us (8%)
  other arithmetic  3.2 us (2%)
    ppermute x16, starting transfers between devices, shifted(): return lax.ppermute(block, axis, route)  64 us
    psum x4, blocking collectives, by_axis(): value = lax.psum(value, axis)  34.3 us
    ppermute x16, waiting for transfers between devices, shifted(): return lax.ppermute(block, axis, route)  33.2 us
    pmin x4, blocking collectives, one_axis_at_a_time(): value = lax.pmin(value, axis)  28.4 us
    unnamed x69, local copies, waits for them, and re-layouts  12 us
    all_gather x1, blocking collectives, turned_gather(): out = lax.all_gather(both, axis, axis=0, tiled=True)  6.99 us
    dot_general x5, matrix products, key_terms_of(): jnp.einsum('hqk,qhd->khd', prob.astype(jnp.bfloat16), by_head(g_rows), pr...  4.77 us
    ppermute x4, local copies, waits for them, and re-layouts, shifted(): return lax.ppermute(block, axis, route)  4.59 us
  transfers between devices with their start and end apart: 16, of which 9 were waited for; matrix products, arithmetic and copies ran while one was open for 8% of the time, Pallas kernels for 0%

commit v1 on v0

--- a/solution.py
+++ b/solution.py
@@ -31,7 +31,7 @@
 
 def by_axis(value, axes):
     for axis in axes:
-        value = lax.psum(value, axis)
+        value = jnp.sum(lax.all_gather(value, axis), axis=0)
     return value
 
 

time: 210 us -> 220 us (1.048)
  blocking collectives: 69.6 us -> 80.3 us
  starting transfers between devices: 64 us -> 61.7 us
    all_gather x0 -> x4, blocking collectives: none -> 44.9 us  [by_axis(): value = jnp.sum(lax.all_gather(value, axis), axis=0)]
    psum x4 -> x0, blocking collectives: 34.3 us -> none  [by_axis(): value = lax.psum(value, axis)]
    ppermute x16, starting transfers between devices: 64 us -> 61.7 us  [shifted(): return lax.ppermute(block, axis, route)]
where the time goes in v1:
time: 220 us; the launch traced here: 218 us
  blocking collectives  80.3 us (36%)
  starting transfers between devices  61.7 us (28%)
  waiting for transfers between devices  33.3 us (15%)
  local copies, waits for them, and re-layouts  19.3 us (9%)
  matrix products  17 us (8%)
  other arithmetic  5.21 us (2%)
    ppermute x16, starting transfers between devices, shifted(): return lax.ppermute(block, axis, route)  61.7 us
    all_gather x4, blocking collectives, by_axis(): value = jnp.sum(lax.all_gather(value, axis), axis=0)  44.9 us
    ppermute x16, waiting for transfers between devices, shifted(): return lax.ppermute(block, axis, route)  33.3 us
    pmin x4, blocking collectives, one_axis_at_a_time(): value = lax.pmin(value, axis)  28.4 us
    unnamed x69, local copies, waits for them, and re-layouts  11.4 us
    all_gather x1, blocking collectives, turned_gather(): out = lax.all_gather(both, axis, axis=0, tiled=True)  7 us
    dot_general x5, matrix products, key_terms_of(): jnp.einsum('hqk,qhd->khd', prob.astype(jnp.bfloat16), by_head(g_rows), pr...  4.77 us
    ppermute x4, local copies, waits for them, and re-layouts, shifted(): return lax.ppermute(block, axis, route)  4.59 us
  transfers between devices with their start and end apart: 16, of which 9 were waited for; matrix products, arithmetic and copies ran while one was open for 8% of the time, Pallas kernels for 0%

profile of v1, /device:TPU:255, one launch (start us, length us, event | category | flops | bytes accessed | tf_op | source)
XLA Modules:
  0.0 218.3 jit_solution(2736696348433483805)
XLA Ops:
  1.8 8.2 %collective-permute-start = (bf16[128,1024]{0,1:T(8,128)(2,1)S(1)}, bf16[128,1024]{0,1:T(8,128)(2,1)S(1)}, u32[]{:S(2)}, u32[]{:S(2)}) collective-permute-start(bf16[128,1024]{0,1:T(8,128)(2,1)S(1)} %copy.331), channel_id=1, source_target_pairs={{0,2},{2,4},{4,6},{6,8},{8,10},{10,12},{12,14},{14,16},{16,18},{18... | collective-permute-start | bytes 786440 | tf_op jit(solution)/shard_map/ppermute | solution.py:47
  12.1 7.0 %all-gather.4 = s32[2,64,2]{1,2,0:T(2,128)S(1)} all-gather(s32[1,64,2]{1,2,0:T(2,128)S(1)} %add_bitcast_fusion), channel_id=1, replica_groups=mesh['seq_0'=8,'seq_1'=4,'seq_2'=4,'seq_3'=2,'head'=2] {'head'}, dimensions={0}, use_global_device_ids=true | all-gather | bytes 1536 | tf_op jit(solution)/shard_map/all_gather | solution.py:22
  19.4 9.4 %pmin.28 = s32[512]{0:T(512)S(1)} all-reduce(s32[512]{0:T(512)S(1)} %select_reduce_fusion.3), channel_id=1, replica_groups=mesh['seq_0'=8,'seq_1'=4,'seq_2'=4,'seq_3'=2,'head'=2] {'seq_0'}, use_global_device_ids=true, to_apply=%region_1.2 | all-reduce | flops 512 | bytes 4096 | tf_op jit(solution)/shard_map/pmin | solution.py:40
  28.7 5.7 %pmin.29 = s32[512]{0:T(512)S(1)} all-reduce(s32[512]{0:T(512)S(1)} %pmin.28), channel_id=1, replica_groups=mesh['seq_0'=8,'seq_1'=4,'seq_2'=4,'seq_3'=2,'head'=2] {'seq_1'}, use_global_device_ids=true, to_apply=%region_2.3 | all-reduce | flops 512 | bytes 4096 | tf_op jit(solution)/shard_map/pmin | solution.py:40
  34.4 4.0 %pmin.30 = s32[512]{0:T(512)S(1)} all-reduce(s32[512]{0:T(512)S(1)} %pmin.29), channel_id=1, replica_groups=mesh['seq_0'=8,'seq_1'=4,'seq_2'=4,'seq_3'=2,'head'=2] {'seq_2'}, use_global_device_ids=true, to_apply=%region_3.4 | all-reduce | flops 512 | bytes 4096 | tf_op jit(solution)/shard_map/pmin | solution.py:40
  38.4 9.3 %pmin.31 = s32[512]{0:T(512)S(1)} all-reduce(s32[512]{0:T(512)S(1)} %pmin.30), channel_id=1, replica_groups=mesh['seq_0'=8,'seq_1'=4,'seq_2'=4,'seq_3'=2,'head'=2] {'seq_3'}, use_global_device_ids=true, to_apply=%region_4.5 | all-reduce | flops 512 | bytes 4096 | tf_op jit(solution)/shard_map/pmin | solution.py:40
  48.1 15.2 %all-gather.5 = f32[8,1,512]{2,1,0:T(1,128)S(1)} all-gather(f32[1,1,512]{2,1,0:T(1,128)S(1)} %bitcast.184), channel_id=2, replica_groups=mesh['seq_0'=8,'seq_1'=4,'seq_2'=4,'seq_3'=2,'head'=2] {'seq_0'}, dimensions={0}, use_global_device_ids=true | all-gather | bytes 18432 | tf_op jit(solution)/shard_map/all_gather | solution.py:34
  63.4 7.3 %all-gather.6 = f32[4,1,512]{2,1,0:T(1,128)S(1)} all-gather(f32[1,1,512]{2,1,0:T(1,128)S(1)} %bitcast.183), channel_id=3, replica_groups=mesh['seq_0'=8,'seq_1'=4,'seq_2'=4,'seq_3'=2,'head'=2] {'seq_1'}, dimensions={0}, use_global_device_ids=true | all-gather | bytes 10240 | tf_op jit(solution)/shard_map/all_gather | solution.py:34
  70.7 9.3 %all-gather.7 = f32[4,1,512]{2,1,0:T(1,128)S(1)} all-gather(f32[1,1,512]{2,1,0:T(1,128)S(1)} %bitcast.185), channel_id=4, replica_groups=mesh['seq_0'=8,'seq_1'=4,'seq_2'=4,'seq_3'=2,'head'=2] {'seq_2'}, dimensions={0}, use_global_device_ids=true | all-gather | bytes 10240 | tf_op jit(solution)/shard_map/all_gather | solution.py:34
  80.0 13.1 %all-gather.8 = f32[2,1,512]{2,1,0:T(1,128)S(1)} all-gather(f32[1,1,512]{2,1,0:T(1,128)S(1)} %bitcast.186), channel_id=5, replica_groups=mesh['seq_0'=8,'seq_1'=4,'seq_2'=4,'seq_3'=2,'head'=2] {'seq_3'}, dimensions={0}, use_global_device_ids=true | all-gather | bytes 6144 | tf_op jit(solution)/shard_map/all_gather | solution.py:34
  93.6 7.8 %collective-permute-start.1 = (bf16[128,1024]{0,1:T(8,128)(2,1)S(1)}, bf16[128,1024]{0,1:T(8,128)(2,1)S(1)}, u32[]{:S(2)}, u32[]{:S(2)}) collective-permute-start(bf16[128,1024]{0,1:T(8,128)(2,1)S(1)} %collective-permute-done), channel_id=1, source_target_pairs={{0,2},{2,4},{4,6},{6,8},{8,10},{10,12},{12,14},{14,16},{16,18},{18... | collective-permute-start | bytes 786440 | tf_op jit(solution)/shard_map/ppermute | solution.py:47
  101.7 2.1 collective-permute-start.5
  104.8 10.4 %collective-permute-start.2 = (bf16[128,1024]{0,1:T(8,128)(2,1)S(1)}, bf16[128,1024]{0,1:T(8,128)(2,1)}, u32[]{:S(2)}, u32[]{:S(2)}) collective-permute-start(bf16[128,1024]{0,1:T(8,128)(2,1)S(1)} %collective-permute-done.1), channel_id=1, source_target_pairs={{0,2},{2,4},{4,6},{6,8},{8,10},{10,12},{12,14},{14,16},{16,18},{18... | collective-permute-start | bytes 786440 | tf_op jit(solution)/shard_map/ppermute | solution.py:47
  115.5 2.5 %collective-permute-start.6 = (bf16[128,1024]{1,0:T(8,128)(2,1)S(1)}, bf16[128,1024]{1,0:T(8,128)(2,1)}, u32[]{:S(2)}, u32[]{:S(2)}) collective-permute-start(bf16[128,1024]{1,0:T(8,128)(2,1)S(1)} %collective-permute-done.5), channel_id=1, source_target_pairs={{0,2},{2,4},{4,6},{6,8},{8,10},{10,12},{12,14},{14,16},{16,18},{18... | collective-permute-start | bytes 786440 | tf_op jit(solution)/shard_map/ppermute | solution.py:47
  118.5 10.5 %collective-permute-start.3 = (bf16[128,1024]{0,1:T(8,128)(2,1)}, bf16[128,1024]{0,1:T(8,128)(2,1)S(1)}, u32[]{:S(2)}, u32[]{:S(2)}) collective-permute-start(bf16[128,1024]{0,1:T(8,128)(2,1)} %collective-permute-done.2), channel_id=1, source_target_pairs={{0,2},{2,4},{4,6},{6,8},{8,10},{10,12},{12,14},{14,16},{16,18},{18... | collective-permute-start | bytes 786440 | tf_op jit(solution)/shard_map/ppermute | solution.py:47
  143.0 2.1 multiply_reduce_fusion
  157.3 2.4 %collective-permute-start.8 = (bf16[128,1024]{1,0:T(8,128)(2,1)S(1)}, bf16[128,1024]{1,0:T(8,128)(2,1)S(1)}, u32[]{:S(2)}, u32[]{:S(2)}) collective-permute-start(bf16[128,1024]{1,0:T(8,128)(2,1)S(1)} %copy.267), channel_id=1, source_target_pairs={{2,0},{4,2},{6,4},{8,6},{10,8},{12,10},{14,12},{16,14},{18,16},{20... | collective-permute-start | bytes 786440 | tf_op jit(solution)/shard_map/ppermute | solution.py:47
  163.7 7.3 %collective-permute-done.8 = bf16[128,1024]{1,0:T(8,128)(2,1)S(1)} collective-permute-done((bf16[128,1024]{1,0:T(8,128)(2,1)S(1)}, bf16[128,1024]{1,0:T(8,128)(2,1)S(1)}, u32[]{:S(2)}, u32[]{:S(2)}) %collective-permute-start.8) | collective-permute-done | bytes 262176 | tf_op jit(solution)/shard_map/ppermute | solution.py:47
  171.1 2.1 collective-permute-start.9
  177.4 7.5 %collective-permute-done.9 = bf16[128,1024]{1,0:T(8,128)(2,1)S(1)} collective-permute-done((bf16[128,1024]{1,0:T(8,128)(2,1)S(1)}, bf16[128,1024]{1,0:T(8,128)(2,1)S(1)}, u32[]{:S(2)}, u32[]{:S(2)}) %collective-permute-start.9) | collective-permute-done | bytes 262176 | tf_op jit(solution)/shard_map/ppermute | solution.py:47
  185.0 2.1 collective-permute-start.10
  192.3 6.5 %collective-permute-done.10 = bf16[128,1024]{1,0:T(8,128)(2,1)S(1)} collective-permute-done((bf16[128,1024]{1,0:T(8,128)(2,1)S(1)}, bf16[128,1024]{1,0:T(8,128)(2,1)S(1)}, u32[]{:S(2)}, u32[]{:S(2)}) %collective-permute-start.10) | collective-permute-done | bytes 262176 | tf_op jit(solution)/shard_map/ppermute | solution.py:47
  209.0 3.7 %collective-permute-done.11 = bf16[128,1024]{1,0:T(8,128)(2,1)S(1)} collective-permute-done((bf16[128,1024]{1,0:T(8,128)(2,1)S(1)}, bf16[128,1024]{1,0:T(8,128)(2,1)S(1)}, u32[]{:S(2)}, u32[]{:S(2)}) %collective-permute-start.11) | collective-permute-done | bytes 262176 | tf_op jit(solution)/shard_map/ppermute | solution.py:47
  213.5 4.0 %collective-permute-done.15 = bf16[128,1024]{1,0:T(8,128)(2,1)S(1)} collective-permute-done((bf16[128,1024]{1,0:T(8,128)(2,1)S(1)}, bf16[128,1024]{1,0:T(8,128)(2,1)S(1)}, u32[]{:S(2)}, u32[]{:S(2)}) %collective-permute-start.15) | collective-permute-done | bytes 262176 | tf_op jit(solution)/shard_map/ppermute | solution.py:47
  (161 shorter events, 57.3 us)
Async XLA Ops:
  0.6 9.4 %copy-start.19 = (bf16[128,1024]{1,0:T(8,128)(2,1)S(1)}, bf16[128,1024]{1,0:T(8,128)(2,1)}, u32[]{:S(2)}) copy-start(bf16[128,1024]{1,0:T(8,128)(2,1)} %param.8) | copy-start | bytes 786436
  0.6 11.4 %copy-start.31 = (s32[64]{0:T(128)S(1)}, s32[64]{0:T(128)}, u32[]{:S(2)}) copy-start(s32[64]{0:T(128)} %param.11) | copy-start | bytes 772
  0.7 11.4 %copy-start.32 = (s32[64]{0:T(128)S(1)}, s32[64]{0:T(128)}, u32[]{:S(2)}) copy-start(s32[64]{0:T(128)} %param.10) | copy-start | bytes 772
  1.8 91.5 %copy-start.13 = (bf16[128,1024]{0,1:T(8,128)(2,1)}, bf16[128,1024]{0,1:T(8,128)(2,1)S(1)}, u32[]{:S(2)}) copy-start(bf16[128,1024]{0,1:T(8,128)(2,1)S(1)} %copy.331) | copy-start | bytes 786436
  1.8 91.3 %copy-start.30 = (bf16[128,1024]{1,0:T(8,128)(2,1)S(1)}, bf16[128,1024]{1,0:T(8,128)(2,1)}, u32[]{:S(2)}) copy-start(bf16[128,1024]{1,0:T(8,128)(2,1)} %param.6) | copy-start | bytes 786436
  1.8 91.8 %collective-permute-start = (bf16[128,1024]{0,1:T(8,128)(2,1)S(1)}, bf16[128,1024]{0,1:T(8,128)(2,1)S(1)}, u32[]{:S(2)}, u32[]{:S(2)}) collective-permute-start(bf16[128,1024]{0,1:T(8,128)(2,1)S(1)} %copy.331), channel_id=1, source_target_pairs={{0,2},{2,4},{4,6},{6,8},{8,10},{10,12},{12,14},{14,16},{16,18},{18... | collective-permute-start | bytes 786440 | tf_op jit(solution)/shard_map/ppermute | solution.py:47
  10.0 91.6 %collective-permute-start.4 = (bf16[128,1024]{1,0:T(8,128)(2,1)S(1)}, bf16[128,1024]{1,0:T(8,128)(2,1)S(1)}, u32[]{:S(2)}, u32[]{:S(2)}) collective-permute-start(bf16[128,1024]{1,0:T(8,128)(2,1)S(1)} %copy-done.19), channel_id=1, source_target_pairs={{0,2},{2,4},{4,6},{6,8},{8,10},{10,12},{12,14},{14,16},{16,18},{18... | collective-permute-start | bytes 786440 | tf_op jit(solution)/shard_map/ppermute | solution.py:47
  93.3 21.9 %copy-start.29 = (bf16[128,1024]{1,0:T(8,128)(2,1)S(1)}, bf16[128,1024]{1,0:T(8,128)(2,1)}, u32[]{:S(2)}) copy-start(bf16[128,1024]{1,0:T(8,128)(2,1)} %param.9) | copy-start | bytes 786436
  93.6 24.4 %copy-start.25 = (bf16[128,1024]{0,1:T(8,128)(2,1)}, bf16[128,1024]{0,1:T(8,128)(2,1)S(1)}, u32[]{:S(2)}) copy-start(bf16[128,1024]{0,1:T(8,128)(2,1)S(1)} %collective-permute-done) | copy-start | bytes 786436
  93.6 11.1 %collective-permute-start.1 = (bf16[128,1024]{0,1:T(8,128)(2,1)S(1)}, bf16[128,1024]{0,1:T(8,128)(2,1)S(1)}, u32[]{:S(2)}, u32[]{:S(2)}) collective-permute-start(bf16[128,1024]{0,1:T(8,128)(2,1)S(1)} %collective-permute-done), channel_id=1, source_target_pairs={{0,2},{2,4},{4,6},{6,8},{8,10},{10,12},{12,14},{14,16},{16,18},{18... | collective-permute-start | bytes 786440 | tf_op jit(solution)/shard_map/ppermute | solution.py:47
  101.7 13.8 %collective-permute-start.5 = (bf16[128,1024]{1,0:T(8,128)(2,1)S(1)}, bf16[128,1024]{1,0:T(8,128)(2,1)S(1)}, u32[]{:S(2)}, u32[]{:S(2)}) collective-permute-start(bf16[128,1024]{1,0:T(8,128)(2,1)S(1)} %collective-permute-done.4), channel_id=1, source_target_pairs={{0,2},{2,4},{4,6},{6,8},{8,10},{10,12},{12,14},{14,16},{16,18},{18... | collective-permute-start | bytes 786440 | tf_op jit(solution)/shard_map/ppermute | solution.py:47
  104.8 24.2 %copy-start.27 = (bf16[128,1024]{0,1:T(8,128)(2,1)}, bf16[128,1024]{0,1:T(8,128)(2,1)S(1)}, u32[]{:S(2)}) copy-start(bf16[128,1024]{0,1:T(8,128)(2,1)S(1)} %collective-permute-done.1) | copy-start | bytes 786436
  104.8 13.7 %collective-permute-start.2 = (bf16[128,1024]{0,1:T(8,128)(2,1)S(1)}, bf16[128,1024]{0,1:T(8,128)(2,1)}, u32[]{:S(2)}, u32[]{:S(2)}) collective-permute-start(bf16[128,1024]{0,1:T(8,128)(2,1)S(1)} %collective-permute-done.1), channel_id=1, source_target_pairs={{0,2},{2,4},{4,6},{6,8},{8,10},{10,12},{12,14},{14,16},{16,18},{18... | collective-permute-start | bytes 786440 | tf_op jit(solution)/shard_map/ppermute | solution.py:47
  115.5 14.6 %collective-permute-start.6 = (bf16[128,1024]{1,0:T(8,128)(2,1)S(1)}, bf16[128,1024]{1,0:T(8,128)(2,1)}, u32[]{:S(2)}, u32[]{:S(2)}) collective-permute-start(bf16[128,1024]{1,0:T(8,128)(2,1)S(1)} %collective-permute-done.5), channel_id=1, source_target_pairs={{0,2},{2,4},{4,6},{6,8},{8,10},{10,12},{12,14},{14,16},{16,18},{18... | collective-permute-start | bytes 786440 | tf_op jit(solution)/shard_map/ppermute | solution.py:47
  118.5 16.6 %collective-permute-start.3 = (bf16[128,1024]{0,1:T(8,128)(2,1)}, bf16[128,1024]{0,1:T(8,128)(2,1)S(1)}, u32[]{:S(2)}, u32[]{:S(2)}) collective-permute-start(bf16[128,1024]{0,1:T(8,128)(2,1)} %collective-permute-done.2), channel_id=1, source_target_pairs={{0,2},{2,4},{4,6},{6,8},{8,10},{10,12},{12,14},{14,16},{16,18},{18... | collective-permute-start | bytes 786440 | tf_op jit(solution)/shard_map/ppermute | solution.py:47
  131.9 9.3 %collective-permute-start.7 = (bf16[128,1024]{1,0:T(8,128)(2,1)}, bf16[128,1024]{1,0:T(8,128)(2,1)}, u32[]{:S(2)}, u32[]{:S(2)}) collective-permute-start(bf16[128,1024]{1,0:T(8,128)(2,1)} %collective-permute-done.6), channel_id=1, source_target_pairs={{0,2},{2,4},{4,6},{6,8},{8,10},{10,12},{12,14},{14,16},{16,18},{18... | collective-permute-start | bytes 786440 | tf_op jit(solution)/shard_map/ppermute | solution.py:47
  157.3 13.7 %collective-permute-start.8 = (bf16[128,1024]{1,0:T(8,128)(2,1)S(1)}, bf16[128,1024]{1,0:T(8,128)(2,1)S(1)}, u32[]{:S(2)}, u32[]{:S(2)}) collective-permute-start(bf16[128,1024]{1,0:T(8,128)(2,1)S(1)} %copy.267), channel_id=1, source_target_pairs={{2,0},{4,2},{6,4},{8,6},{10,8},{12,10},{14,12},{16,14},{18,16},{20... | collective-permute-start | bytes 786440 | tf_op jit(solution)/shard_map/ppermute | solution.py:47
  160.2 13.7 %collective-permute-start.12 = (bf16[128,1024]{1,0:T(8,128)(2,1)S(1)}, bf16[128,1024]{1,0:T(8,128)(2,1)S(1)}, u32[]{:S(2)}, u32[]{:S(2)}) collective-permute-start(bf16[128,1024]{1,0:T(8,128)(2,1)S(1)} %copy.281), channel_id=1, source_target_pairs={{2,0},{4,2},{6,4},{8,6},{10,8},{12,10},{14,12},{16,14},{18,16},{20... | collective-permute-start | bytes 786440 | tf_op jit(solution)/shard_map/ppermute | solution.py:47
  171.1 13.8 %collective-permute-start.9 = (bf16[128,1024]{1,0:T(8,128)(2,1)S(1)}, bf16[128,1024]{1,0:T(8,128)(2,1)S(1)}, u32[]{:S(2)}, u32[]{:S(2)}) collective-permute-start(bf16[128,1024]{1,0:T(8,128)(2,1)S(1)} %add_convert_fusion.7), channel_id=1, source_target_pairs={{2,0},{4,2},{6,4},{8,6},{10,8},{12,10},{14,12},{16,14},{18,16},{20... | collective-permute-start | bytes 786440 | tf_op jit(solution)/shard_map/ppermute | solution.py:47
  174.0 13.9 %collective-permute-start.13 = (bf16[128,1024]{1,0:T(8,128)(2,1)S(1)}, bf16[128,1024]{1,0:T(8,128)(2,1)}, u32[]{:S(2)}, u32[]{:S(2)}) collective-permute-start(bf16[128,1024]{1,0:T(8,128)(2,1)S(1)} %add_convert_fusion.3), channel_id=1, source_target_pairs={{2,0},{4,2},{6,4},{8,6},{10,8},{12,10},{14,12},{16,14},{18,16},{20... | collective-permute-start | bytes 786440 | tf_op jit(solution)/shard_map/ppermute | solution.py:47
  185.0 13.8 %collective-permute-start.10 = (bf16[128,1024]{1,0:T(8,128)(2,1)S(1)}, bf16[128,1024]{1,0:T(8,128)(2,1)S(1)}, u32[]{:S(2)}, u32[]{:S(2)}) collective-permute-start(bf16[128,1024]{1,0:T(8,128)(2,1)S(1)} %add_convert_fusion.6), channel_id=1, source_target_pairs={{2,0},{4,2},{6,4},{8,6},{10,8},{12,10},{14,12},{16,14},{18,16},{20... | collective-permute-start | bytes 786440 | tf_op jit(solution)/shard_map/ppermute | solution.py:47
  188.8 13.8 %collective-permute-start.14 = (bf16[128,1024]{1,0:T(8,128)(2,1)S(1)}, bf16[128,1024]{1,0:T(8,128)(2,1)}, u32[]{:S(2)}, u32[]{:S(2)}) collective-permute-start(bf16[128,1024]{1,0:T(8,128)(2,1)S(1)} %add_convert_fusion.2), channel_id=1, source_target_pairs={{2,0},{4,2},{6,4},{8,6},{10,8},{12,10},{14,12},{16,14},{18,16},{20... | collective-permute-start | bytes 786440 | tf_op jit(solution)/shard_map/ppermute | solution.py:47
  198.9 13.8 %collective-permute-start.11 = (bf16[128,1024]{1,0:T(8,128)(2,1)S(1)}, bf16[128,1024]{1,0:T(8,128)(2,1)S(1)}, u32[]{:S(2)}, u32[]{:S(2)}) collective-permute-start(bf16[128,1024]{1,0:T(8,128)(2,1)S(1)} %add_convert_fusion.5), channel_id=1, source_target_pairs={{2,0},{4,2},{6,4},{8,6},{10,8},{12,10},{14,12},{16,14},{18,16},{20... | collective-permute-start | bytes 786440 | tf_op jit(solution)/shard_map/ppermute | solution.py:47
  203.7 13.8 %collective-permute-start.15 = (bf16[128,1024]{1,0:T(8,128)(2,1)S(1)}, bf16[128,1024]{1,0:T(8,128)(2,1)S(1)}, u32[]{:S(2)}, u32[]{:S(2)}) collective-permute-start(bf16[128,1024]{1,0:T(8,128)(2,1)S(1)} %add_convert_fusion.1), channel_id=1, source_target_pairs={{2,0},{4,2},{6,4},{8,6},{10,8},{12,10},{14,12},{16,14},{18,16},{20... | collective-permute-start | bytes 786440 | tf_op jit(solution)/shard_map/ppermute | solution.py:47
  (25 other events, 68.9 us)
